TPU v7x, 32 devices: a whole 2x2x4 slice. The times are simulated.
32 devices in a mesh: tm: 8 (over z, y), coef: 4 (over x, core).
Axes of the slice: x: 2, y: 2, z: 4, core: 2. Of those that a mesh axis runs over, the one named last changes fastest.
Arguments:
- design: bfloat16 [2048, 50176], P('tm', 'coef'), may hold values from -0.0390625 to 0.0390625
- observed: float32 [2048, 128], P('tm'), may hold values from -6 to 6
- slab_counts: int32 [8], P('tm'), may hold values from 128 to 256, as said below
- gap_mask: int32 [2048], P('tm'), may hold values 0 or 1
- filter_taps: float32 [128], replicated, may hold values from -0.5 to 1.2, as said below
- kaula_diag: float32 [50176], P('coef'), may hold values from 0.1 to 1
- precond: float32 [50176], P('coef'), may hold values from 0.3 to 3
Outputs:
- solution: float32 [50176, 128], P(('coef', 'tm'))
- residual: float32 [50176, 128], P(('coef', 'tm'))
Inputs may be any that keep to these rules, and one draw needn't show every extreme that they name: `slab_counts`: every slab holds at most 256 valid epochs, and some slab holds exactly 256. filter_taps[0] lies between 1 and 1.2.
All inputs are finite; a program needn't handle non-finite values. No bound on the sum of `gap_mask` on one device may be relied on, other than what follows from the above.
Results may differ from a plain program's by a relative error of at most 0.0065.
The roundings to bfloat16 on the way count: a program that leaves them out, or rounds other values in their place, can miss the bound.
Values may be sent and summed in bfloat16 or wider, within the bound.
A program may use at most 64 MiB of HBM per device.

v0:
```python
import jax
import jax.numpy as jnp
from jax import lax
from jax.sharding import PartitionSpec as P

ITERS = 2
HIGHEST = lax.Precision.HIGHEST


def toeplitz(pattern, band_len):
    tiled = jnp.tile(pattern, band_len)[: band_len * (2 * band_len - 1)]
    return tiled.reshape(band_len, 2 * band_len - 1)[:, :band_len]


def block_pair(filter_taps):
    band_len = filter_taps.shape[0]
    spacer = jnp.zeros((band_len,), jnp.float32)
    reversed_taps = filter_taps[:0:-1]
    lower = jnp.concatenate([filter_taps[:1], spacer, reversed_taps])
    upper = jnp.concatenate([jnp.zeros((1,), jnp.float32), reversed_taps, spacer])
    return (toeplitz(lower, band_len), toeplitz(upper, band_len))


def forward(values, lower_block, upper_block):
    band_len = lower_block.shape[0]
    blocks = values.reshape(-1, band_len, values.shape[1])
    previous = jnp.concatenate([jnp.zeros_like(blocks[:1]), blocks[:-1]], 0)
    result = jnp.einsum("ij,bjr->bir", lower_block, blocks, precision=HIGHEST)
    result = result + jnp.einsum("ij,bjr->bir", upper_block, previous, precision=HIGHEST)
    return result.reshape(values.shape)


def backward(values, lower_block, upper_block):
    band_len = lower_block.shape[0]
    blocks = values.reshape(-1, band_len, values.shape[1])
    following = jnp.concatenate([blocks[1:], jnp.zeros_like(blocks[:1])], 0)
    result = jnp.einsum("ji,bjr->bir", lower_block, blocks, precision=HIGHEST)
    result = result + jnp.einsum("ji,bjr->bir", upper_block, following, precision=HIGHEST)
    return result.reshape(values.shape)


def shards(design, observed, slab_counts, gap_mask, filter_taps, kaula_diag, precond):
    epoch_rows, coef_rows = design.shape
    columns = observed.shape[1]
    slabs = lax.axis_size("tm")
    epochs = slabs * epoch_rows
    owned_rows = coef_rows // slabs
    owner_index = lax.axis_index("tm")
    lower_block, upper_block = block_pair(filter_taps)
    position = jnp.arange(epoch_rows, dtype=jnp.int32)
    local_weight = ((gap_mask == 1) & (position < slab_counts[0])).astype(jnp.float32)
    packed = jnp.concatenate([observed, local_weight.reshape(-1, columns)], 0)
    gathered = lax.all_gather(packed, "tm", axis=0, tiled=False)
    all_observed = gathered[:, :epoch_rows].reshape(epochs, columns)
    weight = gathered[:, epoch_rows:].reshape(epochs, 1)
    block = lax.all_to_all(design, "tm", split_axis=1, concat_axis=0, tiled=True)

    def weighted(values):
        inner = forward(weight * values, lower_block, upper_block)
        return (weight * backward(inner, lower_block, upper_block)).astype(jnp.bfloat16)

    def transposed(filtered):
        return lax.dot_general(
            block, filtered, (((0,), (0,)), ((), ())), preferred_element_type=jnp.float32
        )

    def summed(scaled, terms):
        partial = jnp.dot(block, scaled.astype(jnp.bfloat16), preferred_element_type=jnp.float32)
        rows = [jnp.sum(term, 0)[None] for term in terms]
        rows.append(jnp.zeros((8 - len(rows), columns), jnp.float32))
        total = lax.psum(jnp.concatenate([partial] + rows, 0), ("tm", "coef"))
        return (total[:epochs], [total[epochs + at] for at in range(len(terms))])

    start = owner_index * owned_rows
    kaula_col = lax.dynamic_slice_in_dim(kaula_diag, start, owned_rows, 0)[:, None]
    precond_col = lax.dynamic_slice_in_dim(precond, start, owned_rows, 0)[:, None]
    residual = transposed(weighted(all_observed))
    solution = jnp.zeros_like(residual)
    for iteration in range(ITERS):
        scaled = precond_col * residual
        terms = [residual * scaled, kaula_col * scaled * scaled]
        if iteration == 0:
            slab_values, (norm_now, ridge) = summed(scaled, terms)
            direction = scaled
        else:
            terms.append(kaula_col * scaled * direction)
            fresh, (norm_next, own_ridge, cross) = summed(scaled, terms)
            ratio = norm_next / norm_now
            slab_values = fresh + ratio * slab_values
            ridge = own_ridge + ratio * (2.0 * cross + ratio * ridge)
            direction = scaled + ratio * direction
            norm_now = norm_next
        filtered = weighted(slab_values)
        curvature = ridge + jnp.sum(slab_values * filtered.astype(jnp.float32), 0)
        step_len = norm_now / curvature
        image = transposed(filtered) + kaula_col * direction
        solution = solution + step_len * direction
        residual = residual - step_len * image
    return (solution, residual)


def solution(mesh):
    placed = (P("tm", "coef"), P("tm", None), P("tm"), P("tm"), P(), P("coef"), P("coef"))
    return jax.shard_map(
        shards,
        mesh=mesh,
        in_specs=placed,
        out_specs=(P(("coef", "tm"), None), P(("coef", "tm"), None)),
        check_vma=False,
    )
```

profile of v0, /device:TPU:0, one launch (start us, length us, event | category | flops | bytes accessed | tf_op | source)
XLA Modules:
  0.0 508.5 jit_solution(15422720378014263486)
XLA Ops:
  7.2 9.5 %copy.77 = bf16[256,12544]{0,1:T(8,128)(2,1)} copy(bf16[256,12544]{1,0:T(8,128)(2,1)} %param.7) | data formatting | bytes 12845056 | tf_op args[0]
  16.7 7.4 %all-to-all-start = ((bf16[256,8,1568]{0,2,1:T(8,128)(2,1)}), bf16[256,8,1568]{0,2,1:T(8,128)(2,1)}, u32[]{:S(2)}, u32[]{:S(2)}) async-start(bf16[256,8,1568]{0,2,1:T(8,128)(2,1)} %bitcast.147), calls=%async_computation | async-start | bytes 12845056 | tf_op jit(solution)/shard_map/all_to_all | solution.py:56
  28.3 150.4 %all-gather.4.cloned.1.call-done = f32[8,258,128]{2,1,0:T(8,128)} async-done(((f32[1,258,128]{2,1,0:T(8,128)}), f32[8,258,128]{2,1,0:T(8,128)}) %all-gather.4.cloned.1.call-update) | async-done | bytes 1056784 | tf_op jit(solution)/shard_map/all_gather | solution.py:53
  178.8 1.3 slice.97
  181.6 2.1 fusion.19
  183.8 1.7 fusion.8
  185.5 1.1 fusion.42
  186.6 1.1 fusion.10
  187.7 3.7 copy.127
  191.4 1.9 fusion.27
  194.1 1.2 convolution_bitcast_fusion.4
  195.6 1.2 concatenate.38
  197.1 128.1 %all-reduce.9.cloned.1.call-done = f32[2056,128]{0,1:T(8,128)} async-done(((f32[2056,128]{0,1:T(8,128)}), f32[2056,128]{0,1:T(8,128)}) %all-reduce.9.cloned.1.call-update) | async-done | bytes 1052688 | tf_op jit(solution)/shard_map/psum | solution.py:71
  325.2 1.4 slice_multiply_fusion
  328.1 1.7 fusion.7
  329.8 1.1 fusion.41
  330.9 2.0 fusion.18
  332.8 1.3 copy.120
  334.2 2.1 multiply_reduce_fusion.1
  337.3 5.3 %fusion.29 = (f32[128]{0:T(128)S(1)}, f32[128]{0:T(128)S(1)}, f32[128]{0:T(128)S(1)}, f32[1568,128]{1,0:T(8,128)S(1)}) fusion(f32[1568,128]{1,0:T(8,128)} %copy-done.2, f32[1568]{0:T(1024)} %copy-done.10, f32[1568]{0:T(1024)S(1)} %dynamic_slice.6, bf16[2048,1568]{0,1:T(8,128)(2,1)} %bitcast.142, bf16[2048,128]{1,0:T(8,128)(2,1)} %bitcast.166, ...), kind=kOutput, calls=%fused_computation.58 | convolution fusion | flops 824692352 | bytes 8567040 | tf_op jit(solution)/shard_map/dot_general | solution.py:63
  342.6 2.2 convolution_bitcast_fusion.3
  345.2 2.4 concatenate.41
  347.7 130.8 %all-reduce.11.cloned.1.call-done = f32[2056,128]{0,1:T(8,128)} async-done(((f32[2056,128]{0,1:T(8,128)}), f32[2056,128]{0,1:T(8,128)}) %all-reduce.11.cloned.1.call-update) | async-done | bytes 1052688 | tf_op jit(solution)/shard_map/psum | solution.py:71
  479.4 1.4 broadcast_multiply_fusion
  482.9 1.5 copy.94
  484.4 1.7 fusion.6
  487.3 2.2 fusion.17
  489.5 2.6 copy.123
  492.1 1.8 multiply_reduce_fusion
  494.0 1.2 fusion.39
  495.3 1.2 fusion.26
  496.4 5.5 %fusion.5 = f32[1568,128]{1,0:T(8,128)} fusion(f32[1568,128]{1,0:T(8,128)S(1)} %copy-done.5, bf16[2048,1568]{0,1:T(8,128)(2,1)} %bitcast.143, bf16[2048,128]{1,0:T(8,128)(2,1)S(1)} %bitcast.155, f32[1568,128]{1,0:T(8,128)S(1)} %copy-done.3, f32[128]{0:T(128)S(1)} %fusion.44, f32[128]{0:T(128)S(1)} %fusion.39, f32[1568]{0:T(1024)S(1)} %copy-done.11, ...), kind=kOutput, calls=%fused_computation.10 | convolution fusion | flops 823689216 | bytes 9368832 | tf_op jit(solution)/shard_map/dot_general | solution.py:63
  (79 shorter events, 13.2 us)
Async XLA Ops:
  16.7 8.1 %copy-start.14 = (s32[256]{0:T(256)S(1)}, s32[256]{0:T(256)}, u32[]{:S(2)}) copy-start(s32[256]{0:T(256)} %param.10) | copy-start | bytes 3076
  16.7 8.2 %copy-start.9 = (f32[256,128]{1,0:T(8,128)S(1)}, f32[256,128]{1,0:T(8,128)}, u32[]{:S(2)}) copy-start(f32[256,128]{1,0:T(8,128)} %param.8) | copy-start | bytes 393220
  16.7 10.5 %copy-start.15 = (f32[128]{0:T(128)S(1)}, f32[128]{0:T(128)}, u32[]{:S(2)}) copy-start(f32[128]{0:T(128)} %param.11) | copy-start | bytes 1540
  16.7 171.0 %all-to-all-start = ((bf16[256,8,1568]{0,2,1:T(8,128)(2,1)}), bf16[256,8,1568]{0,2,1:T(8,128)(2,1)}, u32[]{:S(2)}, u32[]{:S(2)}) async-start(bf16[256,8,1568]{0,2,1:T(8,128)(2,1)} %bitcast.147), calls=%async_computation | async-start | bytes 12845056 | tf_op jit(solution)/shard_map/all_to_all | solution.py:56
  24.1 154.6 %all-gather.4.cloned.1.call-start = ((), (), s32[]{:S(2)}) async-start(), calls=%async_computation.3 | async-start | bytes 1216512 | tf_op jit(solution)/shard_map/all_gather | solution.py:53
  25.6 299.7 %all-reduce.9.cloned.1.call-start = ((), (), s32[]{:S(2)}) async-start(), calls=%async_computation.1 | async-start | bytes 2228224 | tf_op jit(solution)/shard_map/psum | solution.py:71
  26.4 165.0 %copy-start.10 = (f32[1568]{0:T(1024)}, f32[1568]{0:T(1024)S(1)}, u32[]{:S(2)}) copy-start(f32[1568]{0:T(1024)S(1)} %dynamic_slice.7) | copy-start | bytes 18820
  27.9 157.6 %copy-start.6 = (f32[128,255]{1,0:T(8,128)}, f32[128,255]{1,0:T(8,128)S(1)}, u32[]{:S(2)}) copy-start(f32[128,255]{1,0:T(8,128)S(1)} %reshape.76) | copy-start | bytes 391684
  191.4 2.7 copy-start
  193.4 2.0 copy-start.2
  195.4 131.7 %copy-start.7 = (f32[128,255]{1,0:T(8,128)S(1)}, f32[128,255]{1,0:T(8,128)}, u32[]{:S(2)}) copy-start(f32[128,255]{1,0:T(8,128)} %copy-done.6) | copy-start | bytes 391684
  196.9 281.6 %all-reduce.11.cloned.1.call-start = ((), (), s32[]{:S(2)}) async-start(), calls=%async_computation.2 | async-start | bytes 2228224 | tf_op jit(solution)/shard_map/psum | solution.py:71
  325.2 1.8 copy-start.1
  334.2 8.5 %slice-start = ((s8[6422528]{0:T(1024)(128)(4,1)}), s8[2228224]{0:T(1024)(128)(4,1)S(1)}, s32[]{:S(2)}) async-start(s8[6422528]{0:T(1024)(128)(4,1)} %bitcast.144), calls=%async_computation.4 | async-start | bytes 4456448
  337.3 5.3 %copy-start.12 = (f32[128]{0:T(128)}, f32[128]{0:T(128)S(1)}, u32[]{:S(2)}) copy-start(f32[128]{0:T(128)S(1)} %fusion.38) | copy-start | bytes 1540
  337.3 5.4 %slice-start.1 = ((s8[6422528]{0:T(1024)(128)(4,1)}), s8[4194304]{0:T(1024)(128)(4,1)S(1)}, s32[]{:S(2)}) async-start(s8[6422528]{0:T(1024)(128)(4,1)} %bitcast.144), calls=%async_computation.5 | async-start | bytes 8388608
  342.6 2.3 copy-start.4
  344.9 135.9 %copy-start.8 = (f32[128,255]{1,0:T(8,128)S(1)}, f32[128,255]{1,0:T(8,128)}, u32[]{:S(2)}) copy-start(f32[128,255]{1,0:T(8,128)} %copy-done.6) | copy-start | bytes 391684
  486.2 9.1 %copy-start.3 = (f32[1568,128]{1,0:T(8,128)S(1)}, f32[1568,128]{1,0:T(8,128)}, u32[]{:S(2)}) copy-start(f32[1568,128]{1,0:T(8,128)} %copy-done.2) | copy-start | bytes 2408452
  486.2 9.1 %copy-start.5 = (f32[1568,128]{1,0:T(8,128)S(1)}, f32[1568,128]{1,0:T(8,128)}, u32[]{:S(2)}) copy-start(f32[1568,128]{1,0:T(8,128)} %copy-done.4) | copy-start | bytes 2408452
  486.2 9.1 %copy-start.13 = (f32[128]{0:T(128)S(1)}, f32[128]{0:T(128)}, u32[]{:S(2)}) copy-start(f32[128]{0:T(128)} %copy-done.12) | copy-start | bytes 1540
  487.3 9.1 %copy-start.11 = (f32[1568]{0:T(1024)S(1)}, f32[1568]{0:T(1024)}, u32[]{:S(2)}) copy-start(f32[1568]{0:T(1024)} %copy-done.10) | copy-start | bytes 18820
Sparse Core Ops, SparseCore 0:
  27.7 151.0 all-gather.3
  197.0 128.1 all-reduce.8
  347.8 130.6 all-reduce.10
where the time goes:
time: 510 us; the launch traced here: 509 us
  waiting for transfers between devices  409 us (80%)
  matrix products  33.9 us (7%)
  local copies, waits for them, and re-layouts  31.5 us (6%)
  between operations  14.8 us (3%)
  other arithmetic  11.1 us (2%)
  starting transfers between devices  7.75 us (2%)
    psum x2, waiting for transfers between devices, summed(): total = lax.psum(jnp.concatenate([partial] + rows, 0), ('tm', 'coef'))  259 us
    all_gather x1, waiting for transfers between devices, shards(): gathered = lax.all_gather(packed, 'tm', axis=0, tiled=False)  150 us
    dot_general x3, matrix products, transposed(): lax.dot_general(block, filtered, (((0,), (0,)), ((), ())), preferred_elem...  12.8 us
    unnamed x41, local copies, waits for them, and re-layouts  10.8 us
  transfers between devices with their start and end apart: 4, of which 3 were waited for; matrix products, arithmetic and copies ran while one was open for 2% of the time, Pallas kernels for 0%

commit v1 on v0

--- a/solution.py
+++ b/solution.py
@@ -68,7 +68,7 @@
         partial = jnp.dot(block, scaled.astype(jnp.bfloat16), preferred_element_type=jnp.float32)
         rows = [jnp.sum(term, 0)[None] for term in terms]
         rows.append(jnp.zeros((8 - len(rows), columns), jnp.float32))
-        total = lax.psum(jnp.concatenate([partial] + rows, 0), ("tm", "coef"))
+        total = lax.psum(lax.psum(jnp.concatenate([partial] + rows, 0), "coef"), "tm")
         return (total[:epochs], [total[epochs + at] for at in range(len(terms))])
 
     start = owner_index * owned_rows

time: 510 us -> 485 us (0.951)
  waiting for transfers between devices: 409 us -> 387 us
    psum x2 -> x4, waiting for transfers between devices: 259 us -> 236 us  [the longest x2 166 us: summed(): lax.psum(lax.psum(jnp.concatenate([partial] + rows, 0), 'coef'), 'tm')]
  transfers between devices with their start and end apart: 4 -> 6, of which waited for: 3 -> 5; matrix products, arithmetic and copies ran while one was open for 2% -> 3% of each run, Pallas kernels for 0% -> 0%
where the time goes in v1:
time: 485 us; the launch traced here: 484 us
  waiting for transfers between devices  387 us (80%)
  matrix products  33 us (7%)
  local copies, waits for them, and re-layouts  30.8 us (6%)
  between operations  14.8 us (3%)
  other arithmetic  11.2 us (2%)
  starting transfers between devices  8.05 us (2%)
    psum x2, waiting for transfers between devices, summed(): lax.psum(lax.psum(jnp.concatenate([partial] + rows, 0), 'coef'), 'tm')  166 us
    all_gather x1, waiting for transfers between devices, shards(): gathered = lax.all_gather(packed, 'tm', axis=0, tiled=False)  150 us
    psum x2, waiting for transfers between devices, summed(): lax.psum(jnp.concatenate([partial] + rows, 0), 'coef')  70.2 us
    dot_general x3, matrix products, transposed(): lax.dot_general(block, filtered, (((0,), (0,)), ((), ())), preferred_elem...  12.8 us
    unnamed x41, local copies, waits for them, and re-layouts  11.7 us
  transfers between devices with their start and end apart: 6, of which 5 were waited for; matrix products, arithmetic and copies ran while one was open for 3% of the time, Pallas kernels for 0%

profile of v1, /device:TPU:0, one launch (start us, length us, event | category | flops | bytes accessed | tf_op | source)
XLA Modules:
  0.0 484.4 jit_solution(15101037773644732059)
XLA Ops:
  7.2 9.5 %copy.77 = bf16[256,12544]{0,1:T(8,128)(2,1)} copy(bf16[256,12544]{1,0:T(8,128)(2,1)} %param.7) | data formatting | bytes 12845056 | tf_op args[0]
  16.7 7.4 %all-to-all-start = ((bf16[256,8,1568]{0,2,1:T(8,128)(2,1)}), bf16[256,8,1568]{0,2,1:T(8,128)(2,1)}, u32[]{:S(2)}, u32[]{:S(2)}) async-start(bf16[256,8,1568]{0,2,1:T(8,128)(2,1)} %bitcast.147), calls=%async_computation | async-start | bytes 12845056 | tf_op jit(solution)/shard_map/all_to_all | solution.py:56
  28.3 150.4 %all-gather.4.cloned.1.call-done = f32[8,258,128]{2,1,0:T(8,128)} async-done(((f32[1,258,128]{2,1,0:T(8,128)}), f32[8,258,128]{2,1,0:T(8,128)}) %all-gather.4.cloned.1.call-update) | async-done | bytes 1056784 | tf_op jit(solution)/shard_map/all_gather | solution.py:53
  178.8 1.3 slice.97
  181.6 2.1 fusion.19
  183.8 1.7 fusion.8
  186.6 1.1 fusion.10
  187.7 3.7 copy.127
  191.4 1.9 fusion.27
  194.1 1.2 convolution_bitcast_fusion.4
  195.6 1.2 concatenate.38
  196.9 34.3 %all-reduce.11.cloned.1.call-done = f32[2056,128]{0,1:T(8,128)} async-done(((f32[2056,128]{0,1:T(8,128)}), f32[2056,128]{0,1:T(8,128)}) %all-reduce.11.cloned.1.call-update) | async-done | bytes 1052688 | tf_op jit(solution)/shard_map/psum | solution.py:71
  231.5 82.9 %all-reduce.13.cloned.1.call-done = f32[2056,128]{0,1:T(8,128)} async-done(((f32[2056,128]{0,1:T(8,128)}), f32[2056,128]{0,1:T(8,128)}) %all-reduce.13.cloned.1.call-update) | async-done | bytes 1052688 | tf_op jit(solution)/shard_map/psum | solution.py:71
  314.3 1.3 slice_multiply_fusion
  318.0 1.7 fusion.7
  320.8 1.9 fusion.18
  322.8 1.3 copy.120
  324.1 2.1 multiply_reduce_fusion.1
  327.2 5.3 %fusion.29 = (f32[128]{0:T(128)S(1)}, f32[128]{0:T(128)S(1)}, f32[128]{0:T(128)S(1)}, f32[1568,128]{1,0:T(8,128)S(1)}) fusion(f32[1568,128]{1,0:T(8,128)} %copy-done.2, f32[1568]{0:T(1024)} %copy-done.10, f32[1568]{0:T(1024)S(1)} %dynamic_slice.6, bf16[2048,1568]{0,1:T(8,128)(2,1)} %bitcast.142, bf16[2048,128]{1,0:T(8,128)(2,1)} %bitcast.166, ...), kind=kOutput, calls=%fused_computation.58 | convolution fusion | flops 824692352 | bytes 8567040 | tf_op jit(solution)/shard_map/dot_general | solution.py:63
  332.6 2.3 convolution_bitcast_fusion.3
  335.2 2.2 concatenate.41
  337.6 35.9 %all-reduce.15.cloned.1.call-done = f32[2056,128]{0,1:T(8,128)} async-done(((f32[2056,128]{0,1:T(8,128)}), f32[2056,128]{0,1:T(8,128)}) %all-reduce.15.cloned.1.call-update) | async-done | bytes 1052688 | tf_op jit(solution)/shard_map/psum | solution.py:71
  373.6 83.0 %all-reduce.17.cloned.1.call-done = f32[2056,128]{0,1:T(8,128)} async-done(((f32[2056,128]{0,1:T(8,128)}), f32[2056,128]{0,1:T(8,128)}) %all-reduce.17.cloned.1.call-update) | async-done | bytes 1052688 | tf_op jit(solution)/shard_map/psum | solution.py:71
  457.5 1.4 broadcast_multiply_fusion
  461.0 1.5 copy.94
  462.5 1.7 fusion.6
  465.3 1.1 fusion.17
  466.5 1.3 copy.123
  467.8 2.0 multiply_reduce_fusion
  469.9 1.2 fusion.39
  471.1 1.2 fusion.26
  472.3 5.6 %fusion.5 = f32[1568,128]{1,0:T(8,128)} fusion(f32[1568,128]{1,0:T(8,128)S(1)} %copy-done.5, bf16[2048,1568]{0,1:T(8,128)(2,1)} %bitcast.143, bf16[2048,128]{1,0:T(8,128)(2,1)S(1)} %bitcast.155, f32[1568,128]{1,0:T(8,128)S(1)} %copy-done.3, f32[128]{0:T(128)S(1)} %fusion.44, f32[128]{0:T(128)S(1)} %fusion.39, f32[1568]{0:T(1024)S(1)} %copy-done.11, ...), kind=kOutput, calls=%fused_computation.10 | convolution fusion | flops 823689216 | bytes 9368832 | tf_op jit(solution)/shard_map/dot_general | solution.py:63
  (85 shorter events, 16.6 us)
Async XLA Ops:
  16.7 8.1 %copy-start.14 = (s32[256]{0:T(256)S(1)}, s32[256]{0:T(256)}, u32[]{:S(2)}) copy-start(s32[256]{0:T(256)} %param.10) | copy-start | bytes 3076
  16.7 8.2 %copy-start.9 = (f32[256,128]{1,0:T(8,128)S(1)}, f32[256,128]{1,0:T(8,128)}, u32[]{:S(2)}) copy-start(f32[256,128]{1,0:T(8,128)} %param.8) | copy-start | bytes 393220
  16.7 10.5 %copy-start.15 = (f32[128]{0:T(128)S(1)}, f32[128]{0:T(128)}, u32[]{:S(2)}) copy-start(f32[128]{0:T(128)} %param.11) | copy-start | bytes 1540
  16.7 171.0 %all-to-all-start = ((bf16[256,8,1568]{0,2,1:T(8,128)(2,1)}), bf16[256,8,1568]{0,2,1:T(8,128)(2,1)}, u32[]{:S(2)}, u32[]{:S(2)}) async-start(bf16[256,8,1568]{0,2,1:T(8,128)(2,1)} %bitcast.147), calls=%async_computation | async-start | bytes 12845056 | tf_op jit(solution)/shard_map/all_to_all | solution.py:56
  24.1 154.6 %all-gather.4.cloned.1.call-start = ((), (), s32[]{:S(2)}) async-start(), calls=%async_computation.5 | async-start | bytes 1216512 | tf_op jit(solution)/shard_map/all_gather | solution.py:53
  25.6 205.6 %all-reduce.11.cloned.1.call-start = ((), (), s32[]{:S(2)}) async-start(), calls=%async_computation.1 | async-start | bytes 2228224 | tf_op jit(solution)/shard_map/psum | solution.py:71
  26.4 165.0 %copy-start.10 = (f32[1568]{0:T(1024)}, f32[1568]{0:T(1024)S(1)}, u32[]{:S(2)}) copy-start(f32[1568]{0:T(1024)S(1)} %dynamic_slice.7) | copy-start | bytes 18820
  27.9 157.6 %copy-start.6 = (f32[128,255]{1,0:T(8,128)}, f32[128,255]{1,0:T(8,128)S(1)}, u32[]{:S(2)}) copy-start(f32[128,255]{1,0:T(8,128)S(1)} %reshape.76) | copy-start | bytes 391684
  191.4 2.7 copy-start
  193.4 2.0 copy-start.2
  196.9 117.4 %all-reduce.13.cloned.1.call-start = ((), (), s32[]{:S(2)}) async-start(), calls=%async_computation.2 | async-start | bytes 2228224 | tf_op jit(solution)/shard_map/psum | solution.py:71
  231.2 142.3 %all-reduce.15.cloned.1.call-start = ((), (), s32[]{:S(2)}) async-start(), calls=%async_computation.3 | async-start | bytes 2228224 | tf_op jit(solution)/shard_map/psum | solution.py:71
  315.7 1.2 copy-start.1
  315.8 1.2 copy-start.7
  324.1 8.5 %slice-start = ((s8[6422528]{0:T(1024)(128)(4,1)}), s8[2228224]{0:T(1024)(128)(4,1)S(1)}, s32[]{:S(2)}) async-start(s8[6422528]{0:T(1024)(128)(4,1)} %bitcast.144), calls=%async_computation.6 | async-start | bytes 4456448
  327.2 5.3 %copy-start.12 = (f32[128]{0:T(128)}, f32[128]{0:T(128)S(1)}, u32[]{:S(2)}) copy-start(f32[128]{0:T(128)S(1)} %fusion.38) | copy-start | bytes 1540
  327.2 5.4 %slice-start.1 = ((s8[6422528]{0:T(1024)(128)(4,1)}), s8[4194304]{0:T(1024)(128)(4,1)S(1)}, s32[]{:S(2)}) async-start(s8[6422528]{0:T(1024)(128)(4,1)} %bitcast.144), calls=%async_computation.7 | async-start | bytes 8388608
  332.5 2.3 copy-start.4
  337.4 119.1 %all-reduce.17.cloned.1.call-start = ((), (), s32[]{:S(2)}) async-start(), calls=%async_computation.4 | async-start | bytes 2228224 | tf_op jit(solution)/shard_map/psum | solution.py:71
  457.5 1.5 copy-start.8
  467.8 3.3 copy-start.3
  467.8 3.3 copy-start.5
  467.8 3.3 copy-start.13
  471.1 1.2 copy-start.11
Sparse Core Ops, SparseCore 0:
  27.7 151.0 all-gather.3
  197.0 34.1 all-reduce.10
  234.7 79.5 all-reduce.12
  337.5 35.9 all-reduce.14
  376.9 79.5 all-reduce.16
